TPU v7x, 32 devices: a whole 2x2x4 slice. The times are simulated.
32 devices in a mesh: grp: 2 (over x), lat: 16 (over z, y, core).
Axes of the slice: x: 2, y: 2, z: 4, core: 2. Of those that a mesh axis runs over, the one named last changes fastest.
Arguments:
- acts: bfloat16 [128, 2, 2048], P(('grp', 'lat')), parts along dimension 0, may hold values from -6 to 6
- enc_weight: bfloat16 [4, 2048, 4096], P('grp', None, 'lat'), parts along dimension 0, may hold values from -0.09375 to 0.09375
- enc_bias: float32 [8192], P(('grp', 'lat')), parts along dimension 0, may hold values from -3 to 3
- dec_weight: bfloat16 [4096, 4, 2048], P('lat', 'grp'), parts along dimension 1, may hold values from -0.125 to 0.125
- dec_bias: float32 [4, 2048], P('grp'), parts along dimension 0, may hold values from -5 to 5
Outputs:
- residual: bfloat16 [128, 2, 2048], P(('grp', 'lat')), parts along dimension 0
- grad_enc: bfloat16 [4, 2048, 4096], P('grp', None, 'lat'), parts along dimension 0
- grad_enc_bias: float32 [8192], P(('grp', 'lat')), parts along dimension 0
- grad_dec: bfloat16 [4096, 4, 2048], P('lat', 'grp'), parts along dimension 1
- grad_dec_bias: float32 [4, 2048], P('grp'), parts along dimension 0
There are 2 independent parts, one for each index of `grp`. A program takes and returns all parts, laid end to end along the dimension named above; each array names one. Nothing has to cross between parts.
All inputs are finite; a program needn't handle non-finite values.
Results may differ from a plain program's by a relative error of at most 0.015.
Values may be sent and summed in bfloat16 or wider, within the bound.
No kernel may reach another device: no remote copies, remote signals or barrier semaphores. Data moves between devices by JAX's collectives and lax.ppermute only.
A program may use at most 128 MiB of HBM per device.

v0:
```python
import jax
import jax.numpy as jnp
from jax import lax
from jax.sharding import PartitionSpec as P

sparsity_weight = 2.0


def body(acts, enc_weight, enc_bias, dec_weight, dec_bias):
    tok_dev, layers, width = acts.shape
    lat_dev = enc_weight.shape[2]
    wide = layers * width
    total_rows = tok_dev * lax.axis_size("lat")
    factor = 2.0 / total_rows
    flat_rows = acts.reshape(tok_dev, wide)
    flat_enc = enc_weight.reshape(wide, lat_dev)
    flat_dec = dec_weight.reshape(lat_dev, wide)
    flat_bias = dec_bias.reshape(wide)
    own_start = lax.axis_index("lat") * tok_dev
    gathered = lax.all_gather(flat_rows, "lat", axis=0, tiled=True)
    before = jnp.dot(gathered, flat_enc, preferred_element_type=jnp.float32) + enc_bias
    active = jnp.maximum(before, 0.0).astype(jnp.bfloat16)
    dec_wide = dec_weight.astype(jnp.float32)
    row_sq = jnp.sum(dec_wide * dec_wide, axis=2)
    inv_norm = lax.rsqrt(row_sq + 1.0)
    dec_norm = jnp.sum(jnp.sqrt(row_sq + 1.0), axis=1)
    term = jnp.dot(active, flat_dec, preferred_element_type=jnp.float32)
    own_term = lax.dynamic_slice_in_dim(term, own_start, tok_dev, 0)
    own_term = own_term + flat_bias - flat_rows.astype(jnp.float32)
    term = lax.dynamic_update_slice_in_dim(term, own_term, own_start, 0)
    summed = lax.psum(term, "lat")
    all_residual = summed.astype(jnp.bfloat16)
    own_residual = lax.dynamic_slice_in_dim(all_residual, own_start, tok_dev, 0)
    grad_dec_bias = factor * jnp.sum(all_residual.astype(jnp.float32), axis=0)
    dec_total = lax.dot_general(
        active, all_residual, (((0,), (0,)), ((), ())), preferred_element_type=jnp.float32
    )
    backward = lax.dot_general(
        all_residual, flat_dec, (((1,), (1,)), ((), ())), preferred_element_type=jnp.float32
    )
    grad_act = factor * backward + sparsity_weight / total_rows * dec_norm
    grad_before = jnp.where(before > 0.0, grad_act, 0.0).astype(jnp.bfloat16)
    enc_total = lax.dot_general(
        gathered, grad_before, (((0,), (0,)), ((), ())), preferred_element_type=jnp.float32
    )
    grad_enc = enc_total.astype(jnp.bfloat16).reshape(layers, width, lat_dev)
    grad_enc_bias = jnp.sum(grad_before.astype(jnp.float32), axis=0)
    act_sum = jnp.sum(active.astype(jnp.float32), axis=0)
    grad_dec = (
        factor * dec_total.reshape(lat_dev, layers, width)
        + sparsity_weight / total_rows * act_sum[:, None, None] * dec_wide * inv_norm[:, :, None]
    ).astype(jnp.bfloat16)
    return (
        own_residual.reshape(tok_dev, layers, width),
        grad_enc,
        grad_enc_bias,
        grad_dec,
        grad_dec_bias.reshape(layers, width),
    )


def solution(mesh):
    return jax.shard_map(
        body,
        mesh=mesh,
        in_specs=(
            P(("grp", "lat"), None, None),
            P("grp", None, "lat"),
            P(("grp", "lat")),
            P("lat", "grp", None),
            P("grp", None),
        ),
        out_specs=(
            P(("grp", "lat"), None, None),
            P("grp", None, "lat"),
            P(("grp", "lat")),
            P("lat", "grp", None),
            P("grp", None),
        ),
        check_vma=False,
    )
```

profile of v0, /device:TPU:0, one launch (start us, length us, event | category | flops | bytes accessed | tf_op | source)
XLA Modules:
  0.0 136.5 jit_solution(2590079693091624209)
XLA Ops:
  0.6 0.0 copy-start
  0.7 1.6 %copy-done = bf16[2,2048,256]{2,1,0:T(8,128)(2,1)S(1)} copy-done((bf16[2,2048,256]{2,1,0:T(8,128)(2,1)S(1)}, bf16[2,2048,256]{2,1,0:T(8,128)(2,1)}, u32[]{:S(2)}) %copy-start) | copy-done | bytes 2097176
  2.2 0.7 copy.14
  2.9 0.8 reshape.50
  3.7 0.8 convert_bitcast_fusion
  4.5 0.0 copy-start.3
  4.6 3.8 %fusion.1 = f32[256,2]{1,0:T(8,128)S(1)} fusion(bf16[256,2,2048]{2,1,0:T(2,128)(2,1)} %param.8), kind=kLoop, calls=%fused_computation.5 | loop fusion | flops 3145216 | bytes 2099200 | tf_op jit(solution)/shard_map/reduce_sum | solution.py:24
  8.4 0.1 add_rsqrt_fusion
  8.6 24.6 %all-gather = bf16[16,4,4096]{2,1,0:T(4,128)(2,1)S(1)} all-gather(bf16[1,4,4096]{2,1,0:T(4,128)(2,1)S(1)} %reshape.50), channel_id=1, replica_groups=mesh['grp'=2,'lat'=16] {'lat'}, dimensions={0}, use_global_device_ids=true | all-gather | bytes 557056 | tf_op jit(solution)/shard_map/all_gather | solution.py:20
  33.2 0.1 reshape.51
  33.3 0.0 copy-done.3
  33.3 0.0 copy-start.1
  33.3 0.5 convert_reduce_fusion.1
  33.8 1.1 copy-done.1
  34.9 0.9 copy.13
  35.8 0.0 copy-start.2
  35.8 1.3 copy-done.2
  37.1 1.5 %fusion.8 = f32[64,4096]{1,0:T(8,128)} fusion(bf16[256,4096]{1,0:T(8,128)(2,1)S(1)} %bitcast.21, f32[64,256]{1,0:T(8,128)S(1)} %get-tuple-element.20), kind=kOutput, calls=%fused_computation.26 | convolution fusion | flops 134250496 | bytes 3211264 | tf_op jit(solution)/shard_map/dot_general | solution.py:27
  38.6 1.6 %subtract_dynamic-update-slice_fusion = f32[64,4096]{1,0:T(8,128)} fusion(f32[64,4096]{1,0:T(8,128)} %fusion.8, s32[]{:T(128)S(6)} %select_n.9, f32[4,4096]{1,0:T(4,128)S(1)} %bitcast.24, f32[4096]{0:T(1024)S(1)} %bitcast.25), kind=kLoop, calls=%fused_computation.20 | loop fusion | flops 32768 | bytes 212996 | tf_op jit(solution)/shard_map/dynamic_update_slice | solution.py:30
  40.1 70.1 %all-reduce.1 = bf16[64,4096]{1,0:T(8,128)(2,1)S(1)} all-reduce(f32[64,4096]{1,0:T(8,128)} %subtract_dynamic-update-slice_fusion), channel_id=1, replica_groups=mesh['grp'=2,'lat'=16] {'lat'}, use_global_device_ids=true, to_apply=%region_0.0 | all-reduce | flops 262144 | bytes 1572864 | tf_op jit(solution)/shard_map/psum | solution.py:31
  110.2 2.9 %convert_reduce_fusion.2 = (f32[256]{0:T(256)}, bf16[64,256]{1,0:T(8,128)(2,1)S(1)}) fusion(f32[256]{0:T(256)S(1)} %broadcast_multiply_fusion.2, bf16[64,4096]{1,0:T(8,128)(2,1)S(1)} %all-reduce.1, bf16[256,4096]{1,0:T(8,128)(2,1)} %bitcast.22, f32[64,256]{1,0:T(8,128)S(1)} %get-tuple-element.20), kind=kOutput, calls=%fused_computation.19 | convolution fusion | flops 134332160 | bytes 2721792 | tf_op jit(solution)/shard_map/dot_general | solution.py:38
  113.1 0.1 convert_reduce_fusion
  113.3 0.6 mul.82
  113.9 0.7 reshape.48
  114.6 2.0 %fusion = bf16[4096,256]{0,1:T(8,128)(2,1)} fusion(bf16[64,256]{1,0:T(8,128)(2,1)S(1)} %get-tuple-element.18, bf16[64,4096]{1,0:T(8,128)(2,1)S(1)} %reshape.51), kind=kOutput, calls=%fused_computation.4 | convolution fusion | flops 135266304 | bytes 2654208 | tf_op jit(solution)/shard_map/dot_general | solution.py:43
  116.6 4.1 %copy.12 = bf16[4096,256]{1,0:T(8,128)(2,1)} copy(bf16[4096,256]{0,1:T(8,128)(2,1)} %fusion) | data formatting | bytes 4194304
  120.7 2.7 %convolution_multiply_fusion = f32[256,4096]{1,0:T(8,128)} fusion(bf16[64,4096]{1,0:T(8,128)(2,1)S(1)} %all-reduce.1, f32[64,256]{1,0:T(8,128)S(1)} %get-tuple-element.20), kind=kOutput, calls=%fused_computation | convolution fusion | flops 135299072 | bytes 4784128 | tf_op jit(solution)/shard_map/dot_general | solution.py:35
  123.3 6.6 %mul.74 = f32[256,2,2048]{2,1,0:T(2,128)} reshape(f32[256,4096]{1,0:T(8,128)} %convolution_multiply_fusion) | data formatting | bytes 8388608 | tf_op jit(solution)/shard_map/mul | solution.py:50
  129.9 6.7 %fusion.4 = bf16[256,2,2048]{2,1,0:T(2,128)(2,1)} fusion(f32[256,2,2048]{2,1,0:T(2,128)} %mul.74, bf16[256,2,2048]{2,1,0:T(2,128)(2,1)} %param.8, f32[256]{0:T(256)S(1)} %broadcast_multiply_fusion.1, f32[256,2]{1,0:T(8,128)S(1)} %get-tuple-element.15), kind=kLoop, calls=%fused_computation.8 | loop fusion | flops 5242880 | bytes 8391680 | tf_op jit(solution)/shard_map/convert_element_type | solution.py:52
  (5 shorter events, 0.1 us)
Async XLA Ops:
  0.6 1.6 %copy-start = (bf16[2,2048,256]{2,1,0:T(8,128)(2,1)S(1)}, bf16[2,2048,256]{2,1,0:T(8,128)(2,1)}, u32[]{:S(2)}) copy-start(bf16[2,2048,256]{2,1,0:T(8,128)(2,1)} %param.6) | copy-start | bytes 6291460
  4.5 28.8 %copy-start.3 = (f32[256]{0:T(256)S(1)}, f32[256]{0:T(256)}, u32[]{:S(2)}) copy-start(f32[256]{0:T(256)} %param.7) | copy-start | bytes 3076
  33.3 1.6 %copy-start.1 = (bf16[256,2,2048]{2,1,0:T(2,128)(2,1)S(1)}, bf16[256,2,2048]{2,1,0:T(2,128)(2,1)}, u32[]{:S(2)}) copy-start(bf16[256,2,2048]{2,1,0:T(2,128)(2,1)} %param.8) | copy-start | bytes 6291460
  35.8 1.3 copy-start.2
where the time goes:
time: 137 us
  blocking collectives  94.7 us (69%)
  local copies, waits for them, and re-layouts  18.5 us (14%)
  other arithmetic  13.1 us (10%)
  matrix products  9.56 us (7%)
    psum x1, blocking collectives, body(): summed = lax.psum(term, 'lat')  70.1 us
    all_gather x1, blocking collectives, body(): gathered = lax.all_gather(flat_rows, 'lat', axis=0, tiled=True)  24.6 us
    unnamed x14, local copies, waits for them, and re-layouts  10.6 us
    convert_element_type x1, other arithmetic, body(): grad_dec = (factor * dec_total.reshape(lat_dev, layers, width) + sparsity...  6.65 us
    mul x1, local copies, waits for them, and re-layouts, body(): factor * dec_total.reshape(lat_dev, layers, width)  6.57 us
    reduce_sum x1, other arithmetic, body(): row_sq = jnp.sum(dec_wide * dec_wide, axis=2)  3.84 us
    dot_general x1, matrix products, body(): lax.dot_general(all_residual, flat_dec, (((1,), (1,)), ((), ())), preferr...  2.94 us

commit v1 on v0

--- a/solution.py
+++ b/solution.py
@@ -28,7 +28,8 @@
     own_term = lax.dynamic_slice_in_dim(term, own_start, tok_dev, 0)
     own_term = own_term + flat_bias - flat_rows.astype(jnp.float32)
     term = lax.dynamic_update_slice_in_dim(term, own_term, own_start, 0)
-    summed = lax.psum(term, "lat")
+    pieces = lax.all_gather(term, "lat")
+    summed = jnp.sum(pieces, axis=0)
     all_residual = summed.astype(jnp.bfloat16)
     own_residual = lax.dynamic_slice_in_dim(all_residual, own_start, tok_dev, 0)
     grad_dec_bias = factor * jnp.sum(all_residual.astype(jnp.float32), axis=0)

time: 137 us -> 204 us (1.49)
  waiting for transfers between devices: 0 us -> 120 us
  blocking collectives: 94.7 us -> 24.6 us
  between operations: 0.74 us -> 14.2 us
  other arithmetic: 13.1 us -> 20 us
  matrix products: 9.56 us -> 7.01 us
    all_gather x0 -> x1, waiting for transfers between devices: none -> 120 us  [body(): pieces = lax.all_gather(term, 'lat')]
    psum x1 -> x0, blocking collectives: 70.1 us -> none  [body(): summed = lax.psum(term, 'lat')]
    reduce_sum x0 -> x1, other arithmetic: none -> 6.89 us  [body(): summed = jnp.sum(pieces, axis=0)]
    unnamed x14 -> x19, local copies, waits for them, and re-layouts: 10.6 us -> 9.96 us
  transfers between devices with their start and end apart: 0 -> 1, of which waited for: 0 -> 1; matrix products, arithmetic and copies ran while one was open for 0% -> 2% of each run, Pallas kernels for 0% -> 0%
where the time goes in v1:
time: 204 us
  waiting for transfers between devices  120 us (59%)
  blocking collectives  24.6 us (12%)
  other arithmetic  20 us (10%)
  local copies, waits for them, and re-layouts  17.8 us (9%)
  between operations  14.2 us (7%)
  matrix products  7.01 us (3%)
    all_gather x1, waiting for transfers between devices, body(): pieces = lax.all_gather(term, 'lat')  120 us
    all_gather x1, blocking collectives, body(): gathered = lax.all_gather(flat_rows, 'lat', axis=0, tiled=True)  24.6 us
    unnamed x19, local copies, waits for them, and re-layouts  9.96 us
    reduce_sum x1, other arithmetic, body(): summed = jnp.sum(pieces, axis=0)  6.89 us
    convert_element_type x1, other arithmetic, body(): grad_dec = (factor * dec_total.reshape(lat_dev, layers, width) + sparsity...  6.65 us
    mul x1, local copies, waits for them, and re-layouts, body(): factor * dec_total.reshape(lat_dev, layers, width)  6.57 us
  transfers between devices with their start and end apart: 1, of which 1 were waited for; matrix products, arithmetic and copies ran while one was open for 2% of the time, Pallas kernels for 0%

profile of v1, /device:TPU:0, one launch (start us, length us, event | category | flops | bytes accessed | tf_op | source)
XLA Modules:
  0.0 203.5 jit_solution(15439471231119686037)
XLA Ops:
  7.2 0.0 copy-start
  7.2 0.0 all-gather.3.cloned.1.call-start
  7.2 0.9 reshape.52
  8.2 0.8 convert_bitcast_fusion
  8.9 24.6 %all-gather = bf16[16,4,4096]{2,1,0:T(4,128)(2,1)S(1)} all-gather(bf16[1,4,4096]{2,1,0:T(4,128)(2,1)S(1)} %reshape.52), channel_id=1, replica_groups=mesh['grp'=2,'lat'=16] {'lat'}, dimensions={0}, use_global_device_ids=true | all-gather | bytes 557056 | tf_op jit(solution)/shard_map/all_gather | solution.py:20
  33.6 0.1 reshape.53
  33.7 0.0 copy-start.5
  33.7 2.5 %copy.13 = bf16[32,8,2,2048]{3,1,2,0:T(8,128)(2,1)S(1)} copy(bf16[32,8,2,2048]{3,2,1,0:T(2,128)(2,1)} %bitcast.23) | data formatting | bytes 4194304
  36.2 0.0 copy-start.1
  36.2 0.5 convert_reduce_fusion.1
  36.7 0.0 copy-start.4
  36.7 0.5 fusion.8
  37.2 0.3 copy-done.1
  37.5 1.0 copy-done.3
  38.5 1.0 copy.16
  39.5 0.0 copy-done.4
  39.6 1.6 bitcast_dynamic-update-slice_fusion
  41.1 0.0 all-gather.3.cloned.1.call-update
  41.1 3.8 %fusion.1 = f32[256,2]{1,0:T(8,128)S(1)} fusion(bf16[256,2,2048]{2,1,0:T(2,128)(2,1)} %param.8), kind=kLoop, calls=%fused_computation.5 | loop fusion | flops 3145216 | bytes 2099200 | tf_op jit(solution)/shard_map/reduce_sum | solution.py:24
  45.0 0.1 add_rsqrt_fusion
  45.1 119.9 %all-gather.3.cloned.1.call-done = f32[16,64,4096]{2,1,0:T(8,128)} async-done(((f32[1,64,4096]{2,1,0:T(8,128)}), f32[16,64,4096]{2,1,0:T(8,128)}) %all-gather.3.cloned.1.call-update) | async-done | bytes 16777232 | tf_op jit(solution)/shard_map/all_gather | solution.py:31
  165.0 6.9 %reduce_sum.54 = bf16[64,4096]{1,0:T(8,128)(2,1)S(1)} reduce(f32[16,64,4096]{2,1,0:T(8,128)} %all-gather.3.cloned.1.call-done, f32[]{:T(128)} %constant.7.clone.1), dimensions={0}, to_apply=%region_0.0 | reduce | flops 3932160 | bytes 17301508 | tf_op jit(solution)/shard_map/reduce_sum | solution.py:32
  171.9 0.0 copy-start.2
  171.9 2.7 %convolution_multiply_fusion = f32[256,4096]{1,0:T(8,128)} fusion(bf16[64,4096]{1,0:T(8,128)(2,1)S(1)} %reduce_sum.54, f32[64,256]{1,0:T(8,128)S(1)} %get-tuple-element.20), kind=kOutput, calls=%fused_computation | convolution fusion | flops 135299072 | bytes 4784128 | tf_op jit(solution)/shard_map/dot_general | solution.py:36
  174.6 0.1 convert_reduce_fusion
  174.7 1.3 convert_reduce_fusion.2
  176.0 2.0 %fusion = bf16[4096,256]{0,1:T(8,128)(2,1)} fusion(bf16[64,256]{1,0:T(8,128)(2,1)S(1)} %get-tuple-element.18, bf16[64,4096]{1,0:T(8,128)(2,1)S(1)} %reshape.53), kind=kOutput, calls=%fused_computation.4 | convolution fusion | flops 135266304 | bytes 2654208 | tf_op jit(solution)/shard_map/dot_general | solution.py:44
  178.1 4.1 %copy.12 = bf16[4096,256]{1,0:T(8,128)(2,1)} copy(bf16[4096,256]{0,1:T(8,128)(2,1)} %fusion) | data formatting | bytes 4194304
  182.1 6.6 %mul.74 = f32[256,2,2048]{2,1,0:T(2,128)} reshape(f32[256,4096]{1,0:T(8,128)} %convolution_multiply_fusion) | data formatting | bytes 8388608 | tf_op jit(solution)/shard_map/mul | solution.py:51
  188.7 0.7 reshape.50
  189.4 0.6 mul.82
  190.0 6.7 %fusion.4 = bf16[256,2,2048]{2,1,0:T(2,128)(2,1)} fusion(f32[256,2,2048]{2,1,0:T(2,128)} %mul.74, bf16[256,2,2048]{2,1,0:T(2,128)(2,1)} %param.8, f32[256]{0:T(256)S(1)} %broadcast_multiply_fusion.1, f32[256,2]{1,0:T(8,128)S(1)} %get-tuple-element.15), kind=kLoop, calls=%fused_computation.8 | loop fusion | flops 5242880 | bytes 8391680 | tf_op jit(solution)/shard_map/convert_element_type | solution.py:53
  (10 shorter events, 0.1 us)
Async XLA Ops:
  7.2 29.0 %copy-start = (bf16[2,2048,256]{2,1,0:T(8,128)(2,1)S(1)}, bf16[2,2048,256]{2,1,0:T(8,128)(2,1)}, u32[]{:S(2)}) copy-start(bf16[2,2048,256]{2,1,0:T(8,128)(2,1)} %param.6) | copy-start | bytes 6291460
  7.2 157.8 %all-gather.3.cloned.1.call-start = ((), (), s32[]{:S(2)}) async-start(), calls=%async_computation | async-start | bytes 17825792 | tf_op jit(solution)/shard_map/all_gather | solution.py:31
  33.7 2.5 %copy-start.5 = (f32[256]{0:T(256)S(1)}, f32[256]{0:T(256)}, u32[]{:S(2)}) copy-start(f32[256]{0:T(256)} %param.7) | copy-start | bytes 3076
  36.2 1.3 copy-start.1
  36.7 2.8 %copy-start.4 = (f32[2,2048]{1,0:T(2,128)S(1)}, f32[2,2048]{1,0:T(2,128)}, u32[]{:S(2)}) copy-start(f32[2,2048]{1,0:T(2,128)} %param.9) | copy-start | bytes 49156
  37.5 1.0 copy-start.3
  171.9 2.8 %copy-start.2 = (bf16[32,8,2,2048]{3,1,2,0:T(8,128)(2,1)S(1)}, bf16[32,8,2,2048]{3,1,2,0:T(8,128)(2,1)}, u32[]{:S(2)}) copy-start(bf16[32,8,2,2048]{3,1,2,0:T(8,128)(2,1)} %copy-done.1) | copy-start | bytes 6291460
Sparse Core Ops, SparseCore 0:
  41.3 123.6 all-gather.2
